TPU v7x, 128 devices: a whole 4x4x4 slice. The times are simulated.
128 devices in a mesh: dp: 8 (over x, core), tensor: 16 (over y, z).
Axes of the slice: x: 4, y: 4, z: 4, core: 2. Of those that a mesh axis runs over, the one named last changes fastest.
Arguments:
- hidden: bfloat16 [16, 64, 4608], P('dp', 'tensor'), may hold values from -6 to 6
- gain: float32 [4608], replicated, may hold values from 0.5 to 1.5
- labels: int32 [16, 64], P('dp', 'tensor'), may hold values from 0 to 255999
- lengths: int32 [16], replicated, may hold values from 1 to 64
- embed: bfloat16 [256000, 4608], P(('dp', 'tensor')), may hold values from -0.375 to 0.375
Outputs:
- token_logprob: float32 [16, 64], P('dp', 'tensor')
- mean_nll: float32 [], replicated
- z_loss: float32 [], replicated
All inputs are finite; a program needn't handle non-finite values.
Results may differ from a plain program's by a relative error of at most 0.00058.
Values may be sent and summed in bfloat16 or wider, within the bound.
No kernel may reach another device: no remote copies, remote signals or barrier semaphores. Data moves between devices by JAX's collectives and lax.ppermute only.
A program may use at most 128 MiB of HBM per device.

v0:
```python
import jax
import jax.numpy as jnp
from jax import lax
from jax.sharding import Mesh
from jax.sharding import PartitionSpec as P

CAP = 30
TENSOR = ("tensor_0", "tensor_1")
DP = ("dp_0", "dp_1")
DP_TENSOR = ("dp_0", "dp_1", "tensor_0", "tensor_1")


def joined_along(pieces, dim):
    lengths = list(pieces.shape[1:])
    lengths[dim] *= pieces.shape[0]
    return jnp.moveaxis(pieces, 0, dim).reshape(lengths)


def gather_in_order(value, axes, order):
    pieces = value[None]
    for k in order:
        pieces = lax.all_gather(pieces, axes[k], axis=0, tiled=True)
    block = [lax.axis_size(axes[k]) for k in reversed(order)]
    pieces = pieces.reshape(*block, *value.shape)
    turned = sorted(range(len(order)), key=lambda place: order[len(order) - 1 - place])
    return pieces.transpose(*turned, *range(len(order), pieces.ndim)).reshape(-1, *value.shape)


def gathered_by_axis(value, axes, order, dim):
    return joined_along(gather_in_order(value, axes, order), dim)


def one_axis_at_a_time(value, axes):
    for axis in axes:
        value = lax.psum(value, axis)
    return value


def normalize(rows, gain):
    values = rows.astype(jnp.float32)
    meansq = jnp.mean(values * values, axis=-1, keepdims=True)
    return (values * lax.rsqrt(meansq + 1e-06) * gain).astype(jnp.bfloat16)


def per_device(hidden, gain, labels, lengths, embed):
    n_tensor = lax.axis_size(TENSOR)
    n_all = lax.axis_size(DP) * n_tensor
    seqs, stretch, width = hidden.shape
    vocab_dev = embed.shape[0]
    rows_local = seqs * stretch
    total_rows = rows_local * n_all
    flat = hidden.reshape(rows_local, width)
    row_ids = jnp.arange(total_rows)
    owner = row_ids // rows_local
    within = row_ids % rows_local
    batch_ids = owner // n_tensor * seqs + within // stretch
    positions = owner % n_tensor * stretch + within % stretch
    live_all = (positions < jnp.take(lengths, batch_ids)).astype(jnp.float32)
    all_labels = gathered_by_axis(labels.reshape(rows_local), DP_TENSOR, (0, 2, 3, 1), 0)
    rows = normalize(lax.all_gather(flat, DP_TENSOR, axis=0, tiled=True), gain)
    values = lax.dot_general(
        rows, embed, (((1,), (1,)), ((), ())), preferred_element_type=jnp.float32
    )
    capped = CAP * jnp.tanh(values / CAP)
    sumexp = jnp.sum(jnp.exp(capped), axis=1)
    first = lax.axis_index(DP_TENSOR) * vocab_dev
    local = all_labels - first
    inside = (local >= 0) & (local < vocab_dev)
    chosen = jnp.take_along_axis(capped, jnp.clip(local, 0, vocab_dev - 1)[:, None], axis=1)[:, 0]
    picked = jnp.where(inside, chosen, jnp.float32(0.0))
    own_start = lax.axis_index(DP_TENSOR) * rows_local
    sum_total, pick_total = (
        one_axis_at_a_time(sumexp, DP_TENSOR),
        one_axis_at_a_time(picked, DP_TENSOR),
    )
    own_sum = lax.dynamic_slice_in_dim(sum_total, own_start, rows_local)
    own_pick = lax.dynamic_slice_in_dim(pick_total, own_start, rows_local)
    own_live = lax.dynamic_slice_in_dim(live_all, own_start, rows_local)
    lse = jnp.log(own_sum)
    token = own_live * (own_pick - lse)
    nll_sum, count, square_sum = (
        one_axis_at_a_time(-jnp.sum(token), DP_TENSOR),
        one_axis_at_a_time(jnp.sum(own_live), DP_TENSOR),
        one_axis_at_a_time(jnp.sum(own_live * lse * lse), DP_TENSOR),
    )
    mean_nll = nll_sum / count
    z_loss = 0.01 * square_sum / count
    return (token.reshape(seqs, stretch), mean_nll, z_loss)


def solution(mesh):
    finer = Mesh(mesh.devices.reshape(4, 2, 4, 4), ("dp_0", "dp_1", "tensor_0", "tensor_1"))
    placed = (P(DP, TENSOR, None), P(), P(DP, TENSOR), P(), P(DP_TENSOR, None))
    return jax.shard_map(
        per_device,
        mesh=finer,
        in_specs=placed,
        out_specs=(P(DP, TENSOR), P(), P()),
        check_vma=False,
    )
```

profile of v0, /device:TPU:0, one launch (start us, length us, event | category | flops | bytes accessed | tf_op | source)
XLA Modules:
  0.0 235.7 jit_solution(905636388065802860)
XLA Ops:
  7.2 1.5 reshape.258
  8.8 0.8 reshape.330
  9.5 9.8 %all-gather = s32[4,1,8]{2,1,0:T(1,128)S(1)} all-gather(s32[1,1,8]{2,1,0:T(1,128)S(1)} %reshape.330), channel_id=1, replica_groups=mesh['dp_0'=4,'dp_1'=2,'tensor_0'=4,'tensor_1'=4] {'dp_0'}, dimensions={0}, use_global_device_ids=true | all-gather | bytes 160 | tf_op jit(solution)/shard_map/all_gather | solution.py:22
  19.4 11.3 %all-gather.1 = s32[4,4,8]{2,1,0:T(4,128)S(1)} all-gather(s32[1,4,8]{2,1,0:T(4,128)S(1)} %bitcast.36), channel_id=1, replica_groups=mesh['dp_0'=4,'dp_1'=2,'tensor_0'=4,'tensor_1'=4] {'tensor_0'}, dimensions={0}, use_global_device_ids=true | all-gather | bytes 640 | tf_op jit(solution)/shard_map/all_gather | solution.py:22
  30.7 0.1 copy.22
  30.8 13.2 %all-gather.2 = s32[4,16,8]{1,2,0:T(8,128)S(1)} all-gather(s32[1,16,8]{1,2,0:T(8,128)S(1)} %copy.22), channel_id=1, replica_groups=mesh['dp_0'=4,'dp_1'=2,'tensor_0'=4,'tensor_1'=4] {'tensor_1'}, dimensions={0}, use_global_device_ids=true | all-gather | bytes 2560 | tf_op jit(solution)/shard_map/all_gather | solution.py:22
  44.0 0.1 reshape.336
  44.1 1.8 all-gather.3
  45.9 0.1 copy.26
  46.0 0.1 min.24
  46.1 0.1 min.22
  46.2 0.1 copy.24
  46.4 0.1 and.146
  46.5 0.1 compare_reduce_fusion
  47.0 2.0 fusion.37
  49.0 4.4 %compare_select_fusion.2 = s32[1024,1]{0,1:T(1,128)S(1)} fusion(s32[]{:T(128)} %bitcast.9, s32[]{:T(128)} %bitcast.10, s32[]{:T(128)} %bitcast.11, s32[]{:T(128)} %bitcast.12, s32[]{:T(128)} %bitcast.13, s32[]{:T(128)} %bitcast.15, s32[]{:T(128)} %bitcast.14), kind=kLoop, calls=%fused_computation.22 | loop fusion | flops 60416 | bytes 4124 | tf_op jit(solution)/shard_map/jit(_take)/gather | solution.py:58
  53.5 5.8 %fusion.34 = f32[1024]{0:T(1024)S(1)} fusion(pred[1024]{0:T(1024)(128)(4,1)S(1)} %compare_reduce_fusion, pred[1024]{0:T(1024)(128)(4,1)S(1)} %compare_reduce_fusion.1, pred[1024]{0:T(1024)(128)(4,1)S(1)} %compare_reduce_fusion.2, pred[1024]{0:T(1024)(128)(4,1)S(1)} %compare_reduce_fusion.3, pred[1024]{0:T(1024)(128)(4,1)S(1)} %compare_reduce_fusion.4, ...), kind=kLoop, calls=%fused_computation.90 | loop fusion | flops 73728 | bytes 17444 | tf_op jit(solution)/shard_map/convert_element_type | solution.py:58
  59.3 24.7 %all-gather.6.cloned.1.call-done = bf16[1024,4608]{1,0:T(8,128)(2,1)} async-done(((bf16[8,4608]{1,0:T(8,128)(2,1)}), bf16[1024,4608]{1,0:T(8,128)(2,1)}) %all-gather.6.cloned.1.call-update) | async-done | bytes 9437200 | tf_op jit(solution)/shard_map/all_gather | solution.py:60
  84.0 5.7 %fusion = f32[1024]{0:T(1024)S(1)} fusion(bf16[1024,4608]{1,0:T(8,128)(2,1)} %all-gather.6.cloned.1.call-done), kind=kLoop, calls=%fused_computation.3 | loop fusion | flops 14154752 | bytes 9441280 | tf_op jit(solution)/shard_map/reduce_sum | solution.py:41
  89.7 0.6 copy-done
  90.3 26.1 %exponential_reduce_fusion = (f32[1024]{0:T(1024)S(1)}, f32[1024,2000]{0,1:T(8,128)}) fusion(bf16[2000,4608]{1,0:T(8,128)(2,1)} %param.9, bf16[1024,4608]{1,0:T(8,128)(2,1)S(1)} %copy-done, f32[4608]{0:T(1024)S(1)} %copy-done.1, f32[1024]{0:T(1024)S(1)} %add_rsqrt_fusion), kind=kOutput, calls=%fused_computation.9 | convolution fusion | flops 18899386368 | bytes 36087808 | tf_op jit(solution)/shard_map/dot_general | solution.py:61
  116.4 45.1 %gather_fusion = f32[1024]{0:T(1024)S(1)} fusion(f32[1024,2000]{0,1:T(8,128)} %get-tuple-element.46, s32[1024]{0:T(1024)S(1)} %bitcast.31), kind=kCustom, calls=%fused_computation | custom fusion | bytes 16384 | tf_op jit(solution)/shard_map/jit(take_along_axis)/gather | solution.py:69
  161.5 7.8 %all-reduce.5 = (f32[1024]{0:T(1024)S(1)}, f32[1024]{0:T(1024)S(1)}) all-reduce(f32[1024]{0:T(1024)S(1)} %select_select_fusion.1, f32[1024]{0:T(1024)S(1)} %get-tuple-element.45), channel_id=1, replica_groups=mesh['dp_0'=4,'dp_1'=2,'tensor_0'=4,'tensor_1'=4] {'dp_0'}, use_global_device_ids=true, to_apply=%region_1.2 | all-reduce | flops 2048 | bytes 16384 | tf_op jit(solution)/shard_map/psum | solution.py:35
  169.4 2.5 %all-reduce.7 = (f32[1024]{0:T(1024)S(1)}, f32[1024]{0:T(1024)S(1)}) all-reduce(f32[1024]{0:T(1024)S(1)} %get-tuple-element.18, f32[1024]{0:T(1024)S(1)} %get-tuple-element.19), channel_id=1, replica_groups=mesh['dp_0'=4,'dp_1'=2,'tensor_0'=4,'tensor_1'=4] {'dp_1'}, use_global_device_ids=true, to_apply=%region_2.3 | all-reduce | flops 2048 | bytes 16384 | tf_op jit(solution)/shard_map/psum | solution.py:35
  171.9 8.4 %all-reduce.3 = (f32[1024]{0:T(1024)S(1)}, f32[1024]{0:T(1024)S(1)}) all-reduce(f32[1024]{0:T(1024)S(1)} %get-tuple-element.23, f32[1024]{0:T(1024)S(1)} %get-tuple-element.24), channel_id=1, replica_groups=mesh['dp_0'=4,'dp_1'=2,'tensor_0'=4,'tensor_1'=4] {'tensor_0'}, use_global_device_ids=true, to_apply=%region_3.4 | all-reduce | flops 2048 | bytes 16384 | tf_op jit(solution)/shard_map/psum | solution.py:35
  180.3 10.1 %all-reduce.1 = (f32[1024]{0:T(1024)S(1)}, f32[1024]{0:T(1024)S(1)}) all-reduce(f32[1024]{0:T(1024)S(1)} %get-tuple-element.13, f32[1024]{0:T(1024)S(1)} %get-tuple-element.14), channel_id=1, replica_groups=mesh['dp_0'=4,'dp_1'=2,'tensor_0'=4,'tensor_1'=4] {'tensor_1'}, use_global_device_ids=true, to_apply=%region_4.5 | all-reduce | flops 2048 | bytes 16384 | tf_op jit(solution)/shard_map/psum | solution.py:35
  190.4 0.8 fusion.35
  191.2 0.6 reshape.259
  192.5 8.5 %all-reduce.4 = (f32[]{:T(128)}, f32[]{:T(128)}, f32[]{:T(128)}) all-reduce(f32[]{:T(128)S(6)} %neg.3, f32[]{:T(128)} %get-tuple-element.4, f32[]{:T(128)} %get-tuple-element.3), channel_id=1, replica_groups=mesh['dp_0'=4,'dp_1'=2,'tensor_0'=4,'tensor_1'=4] {'dp_0'}, use_global_device_ids=true, to_apply=%region_11.12 | all-reduce | flops 3 | bytes 24 | tf_op jit(solution)/shard_map/psum | solution.py:35
  201.0 3.1 %all-reduce.6 = (f32[]{:T(128)}, f32[]{:T(128)}, f32[]{:T(128)}) all-reduce(f32[]{:T(128)} %get-tuple-element.15, f32[]{:T(128)} %get-tuple-element.16, f32[]{:T(128)} %get-tuple-element.17), channel_id=1, replica_groups=mesh['dp_0'=4,'dp_1'=2,'tensor_0'=4,'tensor_1'=4] {'dp_1'}, use_global_device_ids=true, to_apply=%region_12.13 | all-reduce | flops 3 | bytes 24 | tf_op jit(solution)/shard_map/psum | solution.py:35
  204.1 10.3 %all-reduce.2 = (f32[]{:T(128)}, f32[]{:T(128)}, f32[]{:T(128)}) all-reduce(f32[]{:T(128)} %get-tuple-element.20, f32[]{:T(128)} %get-tuple-element.21, f32[]{:T(128)} %get-tuple-element.22), channel_id=1, replica_groups=mesh['dp_0'=4,'dp_1'=2,'tensor_0'=4,'tensor_1'=4] {'tensor_0'}, use_global_device_ids=true, to_apply=%region_13.14 | all-reduce | flops 3 | bytes 24 | tf_op jit(solution)/shard_map/psum | solution.py:35
  214.4 9.7 %all-reduce = (f32[]{:T(128)}, f32[]{:T(128)}, f32[]{:T(128)}) all-reduce(f32[]{:T(128)} %get-tuple-element.10, f32[]{:T(128)} %get-tuple-element.11, f32[]{:T(128)} %get-tuple-element.12), channel_id=1, replica_groups=mesh['dp_0'=4,'dp_1'=2,'tensor_0'=4,'tensor_1'=4] {'tensor_1'}, use_global_device_ids=true, to_apply=%region_14.15 | all-reduce | flops 3 | bytes 24 | tf_op jit(solution)/shard_map/psum | solution.py:35
  (24 shorter events, 0.6 us)
Async XLA Ops:
  7.2 82.6 %copy-start.1 = (f32[4608]{0:T(1024)S(1)}, f32[4608]{0:T(1024)}, u32[]{:S(2)}) copy-start(f32[4608]{0:T(1024)} %param.6) | copy-start | bytes 55300
  7.2 76.8 %all-gather.6.cloned.1.call-start = ((), (), s32[]{:S(2)}) async-start(), calls=%async_computation | async-start | bytes 9510912 | tf_op jit(solution)/shard_map/all_gather | solution.py:60
  84.0 6.4 %copy-start = (bf16[1024,4608]{1,0:T(8,128)(2,1)S(1)}, bf16[1024,4608]{1,0:T(8,128)(2,1)}, u32[]{:S(2)}) copy-start(bf16[1024,4608]{1,0:T(8,128)(2,1)} %all-gather.6.cloned.1.call-done) | copy-start | bytes 28311556
Sparse Core Ops, SparseCore 0:
  11.1 72.8 all-gather.5
where the time goes:
time: 237 us; the launch traced here: 236 us
  blocking collectives  96.5 us (41%)
  local copies, waits for them, and re-layouts  51.3 us (22%)
  matrix products  26.1 us (11%)
  waiting for transfers between devices  24.7 us (10%)
  between operations  19.7 us (8%)
  other arithmetic  17.3 us (7%)
    psum x8, blocking collectives, one_axis_at_a_time(): value = lax.psum(value, axis)  60.4 us
    gather x1, local copies, waits for them, and re-layouts, per_device(): jnp.take_along_axis(capped, jnp.clip(local, 0, vocab_dev - 1)[:, None], a...  45.1 us
    all_gather x4, blocking collectives, gather_in_order(): pieces = lax.all_gather(pieces, axes[k], axis=0, tiled=True)  36.2 us
    dot_general x1, matrix products, per_device(): lax.dot_general(rows, embed, (((1,), (1,)), ((), ())), preferred_element_...  26.1 us
    all_gather x1, waiting for transfers between devices, per_device(): rows = normalize(lax.all_gather(flat, DP_TENSOR, axis=0, tiled=True), gain)  24.7 us
    convert_element_type x1, other arithmetic, per_device(): live_all = (positions < jnp.take(lengths, batch_ids)).astype(jnp.float32)  5.82 us
    reduce_sum x1, other arithmetic, normalize(): meansq = jnp.mean(values * values, axis=-1, keepdims=True)  5.72 us
    gather x10, other arithmetic, per_device(): live_all = (positions < jnp.take(lengths, batch_ids)).astype(jnp.float32)  4.91 us
  transfers between devices with their start and end apart: 1, of which 1 were waited for; matrix products, arithmetic and copies ran while one was open for 6% of the time, Pallas kernels for 0%

commit v1 on v0

--- a/solution.py
+++ b/solution.py
@@ -57,7 +57,12 @@
     positions = owner % n_tensor * stretch + within % stretch
     live_all = (positions < jnp.take(lengths, batch_ids)).astype(jnp.float32)
     all_labels = gathered_by_axis(labels.reshape(rows_local), DP_TENSOR, (0, 2, 3, 1), 0)
-    rows = normalize(lax.all_gather(flat, DP_TENSOR, axis=0, tiled=True), gain)
+    rows = normalize(
+        jnp.concatenate(
+            lax.all_to_all(jnp.stack([flat] * lax.axis_size(DP_TENSOR)), DP_TENSOR, 0, 0), axis=0
+        ),
+        gain,
+    )
     values = lax.dot_general(
         rows, embed, (((1,), (1,)), ((), ())), preferred_element_type=jnp.float32
     )

time: 237 us -> 325 us (1.37)
  blocking collectives: 96.5 us -> 208 us
  waiting for transfers between devices: 24.7 us -> 0.01 us
  between operations: 19.7 us -> 6.33 us
  starting transfers between devices: 0.04 us -> 11.6 us
    all_gather x4, blocking collectives: 36.2 us -> 148 us  [gather_in_order(): pieces = lax.all_gather(pieces, axes[k], axis=0, tiled=True)]
    all_gather x1 -> x0, waiting for transfers between devices: 24.7 us -> none  [per_device(): rows = normalize(lax.all_gather(flat, DP_TENSOR, axis=0, tiled=True), gain)]
    all_to_all x0 -> x1, starting transfers between devices: none -> 11.6 us  [per_device(): lax.all_to_all(jnp.stack([flat] * lax.axis_size(DP_TENSOR)), DP_TENSOR, 0...]
    another operation x0 -> x2, local copies, waits for them, and re-layouts: none -> 5.17 us  [per_device(): jnp.stack([flat] * lax.axis_size(DP_TENSOR))]
  transfers between devices with their start and end apart: 1 -> 1, of which waited for: 1 -> 0; matrix products, arithmetic and copies ran while one was open for 6% -> 4% of each run, Pallas kernels for 0% -> 0%
where the time goes in v1:
time: 325 us; the launch traced here: 323 us
  blocking collectives  208 us (64%)
  local copies, waits for them, and re-layouts  52.5 us (16%)
  matrix products  27.9 us (9%)
  other arithmetic  17 us (5%)
  starting transfers between devices  11.6 us (4%)
  between operations  6.33 us (2%)
    all_gather x4, blocking collectives, gather_in_order(): pieces = lax.all_gather(pieces, axes[k], axis=0, tiled=True)  148 us
    psum x8, blocking collectives, one_axis_at_a_time(): value = lax.psum(value, axis)  60.4 us
    gather x1, local copies, waits for them, and re-layouts, per_device(): jnp.take_along_axis(capped, jnp.clip(local, 0, vocab_dev - 1)[:, None], a...  45 us
    dot_general x1, matrix products, per_device(): lax.dot_general(rows, embed, (((1,), (1,)), ((), ())), preferred_element_...  27.9 us
    all_to_all x1, starting transfers between devices, per_device(): lax.all_to_all(jnp.stack([flat] * lax.axis_size(DP_TENSOR)), DP_TENSOR, 0...  11.6 us
  transfers between devices with their start and end apart: 1, of which 0 were waited for; matrix products, arithmetic and copies ran while one was open for 4% of the time, Pallas kernels for 0%

profile of v1, /device:TPU:0, one launch (start us, length us, event | category | flops | bytes accessed | tf_op | source)
XLA Modules:
  0.0 323.5 jit_solution(18150967233153980444)
XLA Ops:
  0.6 0.9 stack_reshape.2
  1.5 4.3 %stack.3 = bf16[128,8,4608]{2,1,0:T(8,128)(2,1)} broadcast(bf16[8,4608]{1,0:T(8,128)(2,1)S(1)} %stack_reshape.2), dimensions={1,2} | broadcast | bytes 9510912 | tf_op jit(solution)/shard_map/stack | solution.py:62
  5.8 11.6 %all-to-all-start = ((bf16[128,8,4608]{2,1,0:T(8,128)(2,1)}), bf16[128,8,4608]{2,1,0:T(8,128)(2,1)}, u32[]{:S(2)}, u32[]{:S(2)}) async-start(bf16[128,8,4608]{2,1,0:T(8,128)(2,1)} %stack.3), calls=%async_computation | async-start | bytes 18874368 | tf_op jit(solution)/shard_map/all_to_all | solution.py:62
  17.5 0.1 reshape.341
  17.6 115.6 %all-gather = s32[4,1,8]{2,1,0:T(1,128)S(1)} all-gather(s32[1,1,8]{2,1,0:T(1,128)S(1)} %reshape.341), channel_id=1, replica_groups=mesh['dp_0'=4,'dp_1'=2,'tensor_0'=4,'tensor_1'=4] {'dp_0'}, dimensions={0}, use_global_device_ids=true | all-gather | bytes 160 | tf_op jit(solution)/shard_map/all_gather | solution.py:22
  133.2 17.9 %all-gather.1 = s32[4,4,8]{2,1,0:T(4,128)S(1)} all-gather(s32[1,4,8]{2,1,0:T(4,128)S(1)} %bitcast.49), channel_id=1, replica_groups=mesh['dp_0'=4,'dp_1'=2,'tensor_0'=4,'tensor_1'=4] {'tensor_0'}, dimensions={0}, use_global_device_ids=true | all-gather | bytes 640 | tf_op jit(solution)/shard_map/all_gather | solution.py:22
  151.1 0.1 copy.28
  151.2 12.4 %all-gather.2 = s32[4,16,8]{1,2,0:T(8,128)S(1)} all-gather(s32[1,16,8]{1,2,0:T(8,128)S(1)} %copy.28), channel_id=1, replica_groups=mesh['dp_0'=4,'dp_1'=2,'tensor_0'=4,'tensor_1'=4] {'tensor_1'}, dimensions={0}, use_global_device_ids=true | all-gather | bytes 2560 | tf_op jit(solution)/shard_map/all_gather | solution.py:22
  163.6 0.1 reshape.347
  163.7 1.8 all-gather.3
  165.5 0.1 copy.32
  165.6 0.1 min.24
  165.8 0.1 min.22
  165.9 0.1 copy.30
  166.0 0.1 and.146
  166.7 0.7 fusion.38
  167.3 4.5 %compare_select_fusion.2 = s32[1024,1]{0,1:T(1,128)S(1)} fusion(s32[]{:T(128)} %bitcast.9, s32[]{:T(128)} %bitcast.10, s32[]{:T(128)} %bitcast.11, s32[]{:T(128)} %bitcast.12, s32[]{:T(128)} %bitcast.13, s32[]{:T(128)} %bitcast.15, s32[]{:T(128)} %bitcast.14), kind=kLoop, calls=%fused_computation.24 | loop fusion | flops 60416 | bytes 4124 | tf_op jit(solution)/shard_map/jit(_take)/gather | solution.py:58
  171.9 5.5 %fusion.35 = f32[1024]{0:T(1024)S(1)} fusion(pred[1024]{0:T(1024)(128)(4,1)S(1)} %compare_reduce_fusion, pred[1024]{0:T(1024)(128)(4,1)S(1)} %compare_reduce_fusion.1, pred[1024]{0:T(1024)(128)(4,1)S(1)} %compare_reduce_fusion.2, pred[1024]{0:T(1024)(128)(4,1)S(1)} %compare_reduce_fusion.3, pred[1024]{0:T(1024)(128)(4,1)S(1)} %compare_reduce_fusion.4, ...), kind=kLoop, calls=%fused_computation.91 | loop fusion | flops 73728 | bytes 17444 | tf_op jit(solution)/shard_map/convert_element_type | solution.py:58
  177.5 5.6 %fusion.3 = f32[128,8]{1,0:T(8,128)S(1)} fusion(bf16[128,8,4608]{2,1,0:T(8,128)(2,1)} %all-to-all-done), kind=kLoop, calls=%fused_computation.6 | loop fusion | flops 14154752 | bytes 9441280 | tf_op jit(solution)/shard_map/reduce_sum | solution.py:41
  183.1 0.1 rsqrt.12
  183.2 27.9 %exponential_reduce_fusion = (f32[1024]{0:T(1024)S(1)}, f32[1024,2000]{0,1:T(8,128)}) fusion(bf16[2000,4608]{1,0:T(8,128)(2,1)} %param.9, bf16[128,8,4608]{2,1,0:T(8,128)(2,1)} %all-to-all-done, f32[4608]{0:T(1024)S(1)} %copy-done.1, f32[1024]{0:T(1024)S(1)} %rsqrt.12), kind=kOutput, calls=%fused_computation.10 | convolution fusion | flops 18899386368 | bytes 36087808 | tf_op jit(solution)/shard_map/dot_general | solution.py:66
  211.1 45.0 %gather_fusion = f32[1024]{0:T(1024)S(1)} fusion(f32[1024,2000]{0,1:T(8,128)} %get-tuple-element.46, s32[1024]{0:T(1024)S(1)} %bitcast.44), kind=kCustom, calls=%fused_computation | custom fusion | bytes 16384 | tf_op jit(solution)/shard_map/jit(take_along_axis)/gather | solution.py:74
  256.2 7.8 %all-reduce.5 = (f32[1024]{0:T(1024)S(1)}, f32[1024]{0:T(1024)S(1)}) all-reduce(f32[1024]{0:T(1024)S(1)} %select_select_fusion.1, f32[1024]{0:T(1024)S(1)} %get-tuple-element.45), channel_id=1, replica_groups=mesh['dp_0'=4,'dp_1'=2,'tensor_0'=4,'tensor_1'=4] {'dp_0'}, use_global_device_ids=true, to_apply=%region_1.2 | all-reduce | flops 2048 | bytes 16384 | tf_op jit(solution)/shard_map/psum | solution.py:35
  264.0 2.5 all-reduce.7
  266.5 7.9 %all-reduce.3 = (f32[1024]{0:T(1024)S(1)}, f32[1024]{0:T(1024)S(1)}) all-reduce(f32[1024]{0:T(1024)S(1)} %get-tuple-element.23, f32[1024]{0:T(1024)S(1)} %get-tuple-element.24), channel_id=1, replica_groups=mesh['dp_0'=4,'dp_1'=2,'tensor_0'=4,'tensor_1'=4] {'tensor_0'}, use_global_device_ids=true, to_apply=%region_3.4 | all-reduce | flops 2048 | bytes 16384 | tf_op jit(solution)/shard_map/psum | solution.py:35
  274.4 10.2 %all-reduce.1 = (f32[1024]{0:T(1024)S(1)}, f32[1024]{0:T(1024)S(1)}) all-reduce(f32[1024]{0:T(1024)S(1)} %get-tuple-element.13, f32[1024]{0:T(1024)S(1)} %get-tuple-element.14), channel_id=1, replica_groups=mesh['dp_0'=4,'dp_1'=2,'tensor_0'=4,'tensor_1'=4] {'tensor_1'}, use_global_device_ids=true, to_apply=%region_4.5 | all-reduce | flops 2048 | bytes 16384 | tf_op jit(solution)/shard_map/psum | solution.py:35
  284.6 0.8 fusion.36
  285.4 0.6 reshape.269
  286.7 10.5 %all-reduce.4 = (f32[]{:T(128)}, f32[]{:T(128)}, f32[]{:T(128)}) all-reduce(f32[]{:T(128)S(6)} %neg.3, f32[]{:T(128)} %get-tuple-element.4, f32[]{:T(128)} %get-tuple-element.3), channel_id=1, replica_groups=mesh['dp_0'=4,'dp_1'=2,'tensor_0'=4,'tensor_1'=4] {'dp_0'}, use_global_device_ids=true, to_apply=%region_11.12 | all-reduce | flops 3 | bytes 24 | tf_op jit(solution)/shard_map/psum | solution.py:35
  297.2 3.1 all-reduce.6
  300.3 9.7 %all-reduce.2 = (f32[]{:T(128)}, f32[]{:T(128)}, f32[]{:T(128)}) all-reduce(f32[]{:T(128)} %get-tuple-element.20, f32[]{:T(128)} %get-tuple-element.21, f32[]{:T(128)} %get-tuple-element.22), channel_id=1, replica_groups=mesh['dp_0'=4,'dp_1'=2,'tensor_0'=4,'tensor_1'=4] {'tensor_0'}, use_global_device_ids=true, to_apply=%region_13.14 | all-reduce | flops 3 | bytes 24 | tf_op jit(solution)/shard_map/psum | solution.py:35
  310.0 8.7 %all-reduce = (f32[]{:T(128)}, f32[]{:T(128)}, f32[]{:T(128)}) all-reduce(f32[]{:T(128)} %get-tuple-element.10, f32[]{:T(128)} %get-tuple-element.11, f32[]{:T(128)} %get-tuple-element.12), channel_id=1, replica_groups=mesh['dp_0'=4,'dp_1'=2,'tensor_0'=4,'tensor_1'=4] {'tensor_1'}, use_global_device_ids=true, to_apply=%region_14.15 | all-reduce | flops 3 | bytes 24 | tf_op jit(solution)/shard_map/psum | solution.py:35
  (27 shorter events, 0.7 us)
Async XLA Ops:
  5.8 11.7 %copy-start.2 = (s32[2,4]{1,0:T(2,128)S(1)}, s32[2,4]{1,0:T(2,128)}, u32[]{:S(2)}) copy-start(s32[2,4]{1,0:T(2,128)} %param.7) | copy-start | bytes 100
  5.8 160.9 %copy-start = (s32[16]{0:T(128)S(1)}, s32[16]{0:T(128)}, u32[]{:S(2)}) copy-start(s32[16]{0:T(128)} %param.8) | copy-start | bytes 196
  5.8 171.7 %all-to-all-start = ((bf16[128,8,4608]{2,1,0:T(8,128)(2,1)}), bf16[128,8,4608]{2,1,0:T(8,128)(2,1)}, u32[]{:S(2)}, u32[]{:S(2)}) async-start(bf16[128,8,4608]{2,1,0:T(8,128)(2,1)} %stack.3), calls=%async_computation | async-start | bytes 18874368 | tf_op jit(solution)/shard_map/all_to_all | solution.py:62
  17.5 165.7 %copy-start.1 = (f32[4608]{0:T(1024)S(1)}, f32[4608]{0:T(1024)}, u32[]{:S(2)}) copy-start(f32[4608]{0:T(1024)} %param.6) | copy-start | bytes 55300
